TPU v7x, 32 devices: a whole 2x2x4 slice. The times are simulated.
32 devices in a mesh: angle: 8 (over y, x, core), scan: 4 (over z).
Axes of the slice: x: 2, y: 2, z: 4, core: 2. Of those that a mesh axis runs over, the one named last changes fastest.
Arguments:
- object_slices: float32 [2, 3, 256, 512], P(None, None, 'scan', 'angle'), may hold values from -5 to 5
- probe: float32 [2, 128, 128], replicated, may hold values from -6 to 6
- intensities: float32 [8, 4, 2, 128, 128], P('angle', 'scan'), may hold values from 0.5 to 3.5
- row_offsets: int32 [8, 4, 2], P('angle', 'scan'), may hold values from 0 to 64
- column_starts: int32 [8, 4, 2], P('angle', 'scan'), may hold values from 0 to 320
- slice_shifts: int32 [8, 3], P('angle'), may hold values from 0 to 64
- counts: int32 [8, 4], P('angle', 'scan'), may hold values from 1 to 2, as said below
Outputs:
- object_gradient: float32 [2, 3, 256, 512], P(None, None, 'scan', 'angle')
- probe_gradient: float32 [2, 128, 128], replicated
Inputs may be any that keep to these rules, and one draw needn't show every extreme that they name: `counts`: the largest value 2 occurs in every draw.
All inputs are finite; a program needn't handle non-finite values.
Results may differ from a plain program's by a relative error of at most 0.0003.
Values sent between devices are 32-bit elements; how exact they have to be, the bound alone decides.
A program may use at most 64 MiB of HBM per device.

v0:
```python
from functools import partial
import jax
import jax.numpy as jnp
from jax import lax
from jax.sharding import PartitionSpec as P


def padded(cells, sides, width):
    for axis, dim in sides:
        count = lax.axis_size(axis)
        ends = count - 1
        head = lax.slice_in_dim(cells, 0, width, axis=dim)
        tail = lax.slice_in_dim(cells, cells.shape[dim] - width, cells.shape[dim], axis=dim)
        cells = jnp.concatenate(
            [
                lax.ppermute(tail, axis, [(i, (i + 1) % count) for i in range(ends)]),
                cells,
                lax.ppermute(head, axis, [((i + 1) % count, i) for i in range(ends)]),
            ],
            axis=dim,
        )
    return cells


def propagator(size):
    index = jnp.arange(size, dtype=jnp.int32)
    centred = ((index + size // 2) % size - size // 2).astype(jnp.float32)
    radius = centred[:, None] * centred[:, None] + centred[None, :] * centred[None, :]
    phase = 8.0 * jnp.pi * radius / (size * size)
    return (jnp.cos(phase), jnp.sin(phase))


def tables(size):
    index = jnp.arange(size, dtype=jnp.int32)
    turns = index[:, None] * index[None, :] % size
    phase = 2.0 * jnp.pi * turns.astype(jnp.float32) / size
    scale = 1.0 / jnp.sqrt(jnp.float32(size))
    return (jnp.cos(phase) * scale, jnp.sin(phase) * scale)


def matmul(first, second):
    return jnp.dot(
        first, second, precision=lax.Precision.HIGHEST, preferred_element_type=jnp.float32
    )


def transform(real_part, imag_part, cosine, sine, sign):
    left_re = matmul(cosine, real_part) - sign * matmul(sine, imag_part)
    left_im = matmul(cosine, imag_part) + sign * matmul(sine, real_part)
    right_re = matmul(left_re, cosine) - sign * matmul(left_im, sine)
    right_im = matmul(left_im, cosine) + sign * matmul(left_re, sine)
    return (right_re, right_im)


def local_loss(slab, probe, measured, weight, cosine, sine, kern_re, kern_im):
    wave_re, wave_im = (probe[0], probe[1])
    layers = slab.shape[1]
    for k in range(layers):
        object_re, object_im = (slab[0, k], slab[1, k])
        wave_re, wave_im = (
            wave_re * object_re - wave_im * object_im,
            wave_re * object_im + wave_im * object_re,
        )
        if k + 1 < layers:
            freq_re, freq_im = transform(wave_re, wave_im, cosine, sine, -1.0)
            freq_re, freq_im = (
                freq_re * kern_re - freq_im * kern_im,
                freq_re * kern_im + freq_im * kern_re,
            )
            wave_re, wave_im = transform(freq_re, freq_im, cosine, sine, 1.0)
    far_re, far_im = transform(wave_re, wave_im, cosine, sine, -1.0)
    differ = far_re * far_re + far_im * far_im - measured
    return weight * jnp.sum(differ * differ)


def local(object_slices, probe, intensities, row_offsets, column_starts, slice_shifts, counts):
    band = object_slices.shape[2]
    framed = padded(object_slices, (("scan", 2),), band)
    region = lax.all_gather(framed, "angle", axis=3, tiled=True)
    size = probe.shape[1]
    slots = row_offsets.shape[2]
    layers = region.shape[1]
    angles = lax.axis_size("angle")
    cosine, sine = tables(size)
    kern_re, kern_im = propagator(size)
    shifts = slice_shifts[0]
    zero = jnp.zeros((), jnp.int32)

    def visit(slot, carry):
        gradient_region, gradient_probe = carry
        top = row_offsets[0, 0, slot]
        start = column_starts[0, 0, slot]
        slab = jnp.concatenate(
            [
                lax.dynamic_slice(
                    region, (zero, zero + k, top, start + shifts[k]), (2, 1, size, size)
                )
                for k in range(layers)
            ],
            axis=1,
        )
        weight = jnp.where(slot < counts[0, 0], 0.5 / angles, 0.0).astype(jnp.float32)
        measured = intensities[0, 0, slot]
        scorer = partial(
            local_loss,
            measured=measured,
            weight=weight,
            cosine=cosine,
            sine=sine,
            kern_re=kern_re,
            kern_im=kern_im,
        )
        loss, pull = jax.vjp(scorer, slab, probe)
        slab_grad, probe_grad = pull(jnp.ones_like(loss))
        for k in range(layers):
            place = (zero, zero + k, top, start + shifts[k])
            current = lax.dynamic_slice(gradient_region, place, (2, 1, size, size))
            gradient_region = lax.dynamic_update_slice(
                gradient_region, current + slab_grad[:, k : k + 1], place
            )
        return (gradient_region, gradient_probe + probe_grad)

    start_carry = (jnp.zeros(region.shape, jnp.float32), jnp.zeros(probe.shape, jnp.float32))
    gradient_region, gradient_probe = lax.fori_loop(0, slots, visit, start_carry)
    shared = lax.psum_scatter(gradient_region, "angle", scatter_dimension=3, tiled=True)
    edges = jnp.concatenate([shared[:, :, :band], shared[:, :, 2 * band :]], axis=2)
    rimmed = padded(edges, (("scan", 2),), band)
    object_gradient = shared[:, :, band : 2 * band] + rimmed[:, :, :band] + rimmed[:, :, 3 * band :]
    group_total = lax.psum(gradient_probe, "scan")
    probe_gradient = lax.psum(group_total, "angle")
    return (object_gradient, probe_gradient)


def solution(mesh):
    return jax.shard_map(
        local,
        mesh=mesh,
        in_specs=(
            P(None, None, "scan", "angle"),
            P(),
            P("angle", "scan", None, None, None),
            P("angle", "scan", None),
            P("angle", "scan", None),
            P("angle", None),
            P("angle", "scan"),
        ),
        out_specs=(P(None, None, "scan", "angle"), P()),
        check_vma=False,
    )
```

profile of v0, /device:TPU:0, one launch (start us, length us, event | category | flops | bytes accessed | tf_op | source)
XLA Modules:
  0.0 352.9 jit_solution(17662193562692884179)
XLA Ops:
  7.2 1.1 copy.25
  8.3 1.3 collective-permute-start.1
  9.6 5.6 %collective-permute-start = (f32[2,3,64,64]{2,0,1,3:T(2,128)S(1)}, f32[2,3,64,64]{2,0,1,3:T(2,128)S(1)}, u32[]{:S(2)}, u32[]{:S(2)}) collective-permute-start(f32[2,3,64,64]{2,0,1,3:T(2,128)S(1)} %copy.25), channel_id=1, source_target_pairs={{0,1},{1,2},{2,3},{4,5},{5,6},{6,7},{8,9},{9,10},{10,11},{12,13},{... | collective-permute-start | bytes 294920 | tf_op jit(solution)/shard_map/ppermute | solution.py:16
  15.2 2.9 collective-permute-done.1
  18.2 1.2 collective-permute-done
  19.3 1.2 pad_maximum_fusion
  20.7 34.6 %all-gather.2.cloned.1.call-done = f32[2,3,192,512]{2,0,1,3:T(2,128)} async-done(((f32[2,3,192,64]{2,0,1,3:T(2,128)}), f32[2,3,192,512]{2,0,1,3:T(2,128)}) %all-gather.2.cloned.1.call-update) | async-done | bytes 2359312 | tf_op jit(solution)/shard_map/all_gather | solution.py:79
  55.2 5.6 %copy.28 = f32[2,3,192,512]{3,2,1,0:T(8,128)} copy(f32[2,3,192,512]{2,0,1,3:T(2,128)} %all-gather.2.cloned.1.call-done) | data formatting | bytes 4718592
  61.8 137.1 %while.19 = (s32[]{:T(128)}, f32[2,3,192,512]{3,2,1,0:T(8,128)S(1)}, f32[2,128,128]{2,1,0:T(8,128)S(1)}, s32[1,1,2]{2,1,0:T(1,128)S(1)}, s32[1,1,2]{2,1,0:T(1,12...) while((s32[]{:T(128)}, ...), condition=%wide.region_1.2_spmd.clone.clone.clone.clone, body=%wide.region_0.1_spmd.clone.clone.clone.clone.sunk | while | flops 2037301248 | bytes 20128300 | solution.py:124
  69.6 1.1 fusion.857
  74.6 0.8 fusion.868
  75.5 0.8 convolution_add_fusion.36
  76.8 0.8 fusion.866
  77.6 0.8 convolution_subtract_fusion.8
  79.3 1.5 multiply_add_fusion.7
  84.7 0.8 fusion.880
  85.5 1.3 convolution_add_fusion.37
  87.3 0.8 fusion.878
  88.2 0.8 convolution_subtract_fusion.10
  89.9 1.5 multiply_subtract_fusion.3
  99.0 1.5 add_bitcast_fusion.9
  104.8 0.8 fusion.902
  105.6 0.8 convolution_add_fusion.43
  107.2 0.8 convolution_add_fusion.42
  109.5 1.5 add_bitcast_fusion.10
  115.2 0.8 fusion.913
  116.0 0.8 convolution_add_fusion.47
  117.5 0.8 convolution_add_fusion.46
  120.1 1.5 add_bitcast_fusion.11
  121.8 2.3 dynamic_update_slice.36
  124.3 2.3 dynamic_update_slice.37
  126.7 2.3 dynamic_update_slice.38
  137.1 1.1 fusion.857
  142.1 0.8 fusion.868
  142.9 0.8 convolution_add_fusion.36
  144.2 0.8 fusion.866
  145.0 0.8 convolution_subtract_fusion.8
  146.8 1.5 multiply_add_fusion.7
  152.2 0.8 fusion.880
  153.0 1.0 convolution_add_fusion.37
  154.5 0.8 fusion.878
  155.3 0.8 convolution_subtract_fusion.10
  157.0 1.5 multiply_subtract_fusion.3
  166.1 1.5 add_bitcast_fusion.9
  172.0 0.8 fusion.902
  172.7 0.8 convolution_add_fusion.43
  174.3 0.8 convolution_add_fusion.42
  176.7 1.5 add_bitcast_fusion.10
  182.3 0.8 fusion.913
  184.7 0.8 convolution_add_fusion.46
  186.5 0.9 fusion.914
  187.4 1.5 add_bitcast_fusion.11
  189.2 2.3 dynamic_update_slice.36
  191.6 2.3 dynamic_update_slice.37
  194.0 2.3 dynamic_update_slice.38
  199.0 3.4 copy.37
  202.4 6.0 %reshape.42 = f32[512,1152]{1,0:T(8,128)} reshape(f32[512,2,3,192]{3,2,1,0:T(4,128)} %bitcast.367) | data formatting | bytes 4718592
  209.2 41.8 %reduce-scatter.4.cloned.1.call-done = f32[64,1152]{1,0:T(8,128)} async-done(((f32[512,1152]{1,0:T(8,128)}), f32[64,1152]{1,0:T(8,128)}) %reduce-scatter.4.cloned.1.call-update) | async-done | bytes 294928
  250.9 1.3 reshape.43
  252.8 1.3 collective-permute-start.3
  254.1 4.6 %collective-permute-start.2 = (f32[2,3,64,64]{3,2,1,0:T(8,128)S(1)}, f32[2,3,64,64]{3,2,1,0:T(8,128)S(1)}, u32[]{:S(2)}, u32[]{:S(2)}) collective-permute-start(f32[2,3,64,64]{3,2,1,0:T(8,128)S(1)} %copy.40), channel_id=1, source_target_pairs={{0,1},{1,2},{2,3},{4,5},{5,6},{6,7},{8,9},{9,10},{10,11},{12,13},{... | collective-permute-start | bytes 294920 | tf_op jit(solution)/shard_map/ppermute | solution.py:16
  258.6 29.9 %all-reduce.11.cloned.1.call-done = f32[2,128,128]{2,1,0:T(8,128)} async-done(((f32[2,128,128]{2,1,0:T(8,128)}), f32[2,128,128]{2,1,0:T(8,128)}) %all-reduce.11.cloned.1.call-update) | async-done | bytes 131088 | tf_op jit(solution)/shard_map/psum | solution.py:129
  289.4 55.2 %all-reduce.13.cloned.1.call-done = f32[2,128,128]{2,1,0:T(8,128)} async-done(((f32[2,128,128]{2,1,0:T(8,128)}), f32[2,128,128]{2,1,0:T(8,128)}) %all-reduce.13.cloned.1.call-update) | async-done | bytes 131088 | tf_op jit(solution)/shard_map/psum | solution.py:130
  344.6 1.6 copy.56
  (166 shorter events, 69.4 us)
Async XLA Ops:
  7.2 48.1 %all-gather.2.cloned.1.call-start = ((), (), s32[]{:S(2)}) async-start(), calls=%async_computation.1 | async-start | bytes 3538944 | tf_op jit(solution)/shard_map/all_gather | solution.py:79
  8.3 9.9 %collective-permute-start.1 = (f32[2,3,64,64]{2,0,1,3:T(2,128)S(1)}, f32[2,3,64,64]{2,0,1,3:T(2,128)S(1)}, u32[]{:S(2)}, u32[]{:S(2)}) collective-permute-start(f32[2,3,64,64]{2,0,1,3:T(2,128)S(1)} %copy.25), channel_id=1, source_target_pairs={{1,0},{2,1},{3,2},{5,4},{6,5},{7,6},{9,8},{10,9},{11,10},{13,12},{... | collective-permute-start | bytes 294920 | tf_op jit(solution)/shard_map/ppermute | solution.py:18
  9.6 9.7 %collective-permute-start = (f32[2,3,64,64]{2,0,1,3:T(2,128)S(1)}, f32[2,3,64,64]{2,0,1,3:T(2,128)S(1)}, u32[]{:S(2)}, u32[]{:S(2)}) collective-permute-start(f32[2,3,64,64]{2,0,1,3:T(2,128)S(1)} %copy.25), channel_id=1, source_target_pairs={{0,1},{1,2},{2,3},{4,5},{5,6},{6,7},{8,9},{9,10},{10,11},{12,13},{... | collective-permute-start | bytes 294920 | tf_op jit(solution)/shard_map/ppermute | solution.py:16
  20.6 230.3 %reduce-scatter.4.cloned.1.call-start = ((), (), s32[]{:S(2)}) async-start(), calls=%async_computation.4 | async-start | bytes 2654208
  60.8 0.9 copy-start
  60.8 0.9 copy-start.2
  60.8 0.9 copy-start.3
  60.8 0.9 copy-start.4
  60.8 1.0 copy-start.5
  199.0 3.4 copy-start.1
  208.4 80.1 %all-reduce.11.cloned.1.call-start = ((), (), s32[]{:S(2)}) async-start(), calls=%async_computation.2 | async-start | bytes 262144 | tf_op jit(solution)/shard_map/psum | solution.py:129
  209.1 135.5 %all-reduce.13.cloned.1.call-start = ((), (), s32[]{:S(2)}) async-start(), calls=%async_computation.3 | async-start | bytes 262144 | tf_op jit(solution)/shard_map/psum | solution.py:130
  252.8 35.9 %collective-permute-start.3 = (f32[2,3,64,64]{3,2,1,0:T(8,128)S(1)}, f32[2,3,64,64]{3,2,1,0:T(8,128)S(1)}, u32[]{:S(2)}, u32[]{:S(2)}) collective-permute-start(f32[2,3,64,64]{3,2,1,0:T(8,128)S(1)} %copy.41), channel_id=1, source_target_pairs={{1,0},{2,1},{3,2},{5,4},{6,5},{7,6},{9,8},{10,9},{11,10},{13,12},{... | collective-permute-start | bytes 294920 | tf_op jit(solution)/shard_map/ppermute | solution.py:18
  254.1 34.6 %collective-permute-start.2 = (f32[2,3,64,64]{3,2,1,0:T(8,128)S(1)}, f32[2,3,64,64]{3,2,1,0:T(8,128)S(1)}, u32[]{:S(2)}, u32[]{:S(2)}) collective-permute-start(f32[2,3,64,64]{3,2,1,0:T(8,128)S(1)} %copy.40), channel_id=1, source_target_pairs={{0,1},{1,2},{2,3},{4,5},{5,6},{6,7},{8,9},{9,10},{10,11},{12,13},{... | collective-permute-start | bytes 294920 | tf_op jit(solution)/shard_map/ppermute | solution.py:16
Sparse Core Ops, SparseCore 0:
  20.7 34.4 all-gather.1
  208.5 42.3 reduce-scatter.3
  253.8 34.6 all-reduce.10
  291.4 53.1 all-reduce.12
where the time goes:
time: 356 us; the launch traced here: 353 us
  waiting for transfers between devices  166 us (47%)
  matrix products  101 us (28%)
  local copies, waits for them, and re-layouts  36.8 us (10%)
  loops' own time  16.9 us (5%)
  between operations  14.1 us (4%)
  starting transfers between devices  12.9 us (4%)
  other arithmetic  4.94 us (1%)
    dot_general x160, matrix products, matmul(): jnp.dot(first, second, precision=lax.Precision.HIGHEST, preferred_element...  101 us
    psum x1, waiting for transfers between devices, local(): probe_gradient = lax.psum(group_total, 'angle')  55.2 us
    unnamed x5, waiting for transfers between devices  42.5 us
    all_gather x1, waiting for transfers between devices, local(): region = lax.all_gather(framed, 'angle', axis=3, tiled=True)  34.6 us
    psum x1, waiting for transfers between devices, local(): group_total = lax.psum(gradient_probe, 'scan')  29.9 us
    unnamed x21, local copies, waits for them, and re-layouts  20 us
    another operation x1, loops' own time, local(): lax.fori_loop(0, slots, visit, start_carry)  16.9 us
    dynamic_update_slice x6, local copies, waits for them, and re-layouts, visit(): lax.dynamic_update_slice(gradient_region, current + slab_grad[:, k:k + 1]...  13.8 us
  transfers between devices with their start and end apart: 8, of which 6 were waited for; matrix products, arithmetic and copies ran while one was open for 1% of the time, Pallas kernels for 0%

commit v1 on v0

--- a/solution.py
+++ b/solution.py
@@ -3,6 +3,15 @@
 import jax.numpy as jnp
 from jax import lax
 from jax.sharding import PartitionSpec as P
+
+
+def sum_by_hops(shard, mesh_axis):
+    devices = lax.axis_size(mesh_axis)
+    total, reach = (shard, 1)
+    while reach < devices:
+        total = total + lax.ppermute(total, mesh_axis, [(i, i ^ reach) for i in range(devices)])
+        reach = 2 * reach
+    return total
 
 
 def padded(cells, sides, width):
@@ -126,7 +135,7 @@
     edges = jnp.concatenate([shared[:, :, :band], shared[:, :, 2 * band :]], axis=2)
     rimmed = padded(edges, (("scan", 2),), band)
     object_gradient = shared[:, :, band : 2 * band] + rimmed[:, :, :band] + rimmed[:, :, 3 * band :]
-    group_total = lax.psum(gradient_probe, "scan")
+    group_total = sum_by_hops(gradient_probe, "scan")
     probe_gradient = lax.psum(group_total, "angle")
     return (object_gradient, probe_gradient)
 

time: 356 us -> 324 us (0.910)
  waiting for transfers between devices: 166 us -> 129 us
  starting transfers between devices: 12.9 us -> 16.5 us
    psum x1 -> x0, waiting for transfers between devices: 29.9 us -> none  [local(): group_total = lax.psum(gradient_probe, 'scan')]
    unnamed x5 -> x4, waiting for transfers between devices: 42.5 us -> 34.8 us
    psum x1, waiting for transfers between devices: 55.2 us -> 49 us  [local(): probe_gradient = lax.psum(group_total, 'angle')]
    ppermute x0 -> x2, waiting for transfers between devices: none -> 4.06 us  [sum_by_hops(): lax.ppermute(total, mesh_axis, [(i, i ^ reach) for i in range(devices)])]
    ppermute x0 -> x2, starting transfers between devices: none -> 3.67 us  [sum_by_hops(): lax.ppermute(total, mesh_axis, [(i, i ^ reach) for i in range(devices)])]
    unnamed x21 -> x19, local copies, waits for them, and re-layouts: 20 us -> 20.1 us
  transfers between devices with their start and end apart: 8 -> 9, of which waited for: 6 -> 8; matrix products, arithmetic and copies ran while one was open for 1% -> 1% of each run, Pallas kernels for 0% -> 0%
where the time goes in v1:
time: 324 us; the launch traced here: 321 us
  waiting for transfers between devices  129 us (40%)
  matrix products  101 us (31%)
  local copies, waits for them, and re-layouts  37 us (11%)
  loops' own time  17.5 us (5%)
  starting transfers between devices  16.5 us (5%)
  between operations  14.1 us (4%)
  other arithmetic  5.62 us (2%)
    dot_general x160, matrix products, matmul(): jnp.dot(first, second, precision=lax.Precision.HIGHEST, preferred_element...  101 us
    psum x1, waiting for transfers between devices, local(): probe_gradient = lax.psum(group_total, 'angle')  49 us
    unnamed x4, waiting for transfers between devices  34.8 us
    all_gather x1, waiting for transfers between devices, local(): region = lax.all_gather(framed, 'angle', axis=3, tiled=True)  34.6 us
    unnamed x19, local copies, waits for them, and re-layouts  20.1 us
    another operation x1, loops' own time, local(): lax.fori_loop(0, slots, visit, start_carry)  17.5 us
    dynamic_update_slice x6, local copies, waits for them, and re-layouts, visit(): lax.dynamic_update_slice(gradient_region, current + slab_grad[:, k:k + 1]...  13.8 us
    ppermute x2, starting transfers between devices, padded(): lax.ppermute(tail, axis, [(i, (i + 1) % count) for i in range(ends)])  10.2 us
  transfers between devices with their start and end apart: 9, of which 8 were waited for; matrix products, arithmetic and copies ran while one was open for 1% of the time, Pallas kernels for 0%

profile of v1, /device:TPU:0, one launch (start us, length us, event | category | flops | bytes accessed | tf_op | source)
XLA Modules:
  0.0 321.1 jit_solution(14854042974119993961)
XLA Ops:
  7.2 1.1 copy.25
  8.3 1.3 collective-permute-start.1
  9.6 5.6 %collective-permute-start = (f32[2,3,64,64]{2,0,1,3:T(2,128)S(1)}, f32[2,3,64,64]{2,0,1,3:T(2,128)S(1)}, u32[]{:S(2)}, u32[]{:S(2)}) collective-permute-start(f32[2,3,64,64]{2,0,1,3:T(2,128)S(1)} %copy.25), channel_id=1, source_target_pairs={{0,1},{1,2},{2,3},{4,5},{5,6},{6,7},{8,9},{9,10},{10,11},{12,13},{... | collective-permute-start | bytes 294920 | tf_op jit(solution)/shard_map/ppermute | solution.py:25
  15.2 2.9 collective-permute-done.1
  18.2 1.2 collective-permute-done
  19.3 1.2 pad_maximum_fusion
  20.6 34.6 %all-gather.2.cloned.1.call-done = f32[2,3,192,512]{2,0,1,3:T(2,128)} async-done(((f32[2,3,192,64]{2,0,1,3:T(2,128)}), f32[2,3,192,512]{2,0,1,3:T(2,128)}) %all-gather.2.cloned.1.call-update) | async-done | bytes 2359312 | tf_op jit(solution)/shard_map/all_gather | solution.py:88
  55.2 5.6 %copy.28 = f32[2,3,192,512]{3,2,1,0:T(8,128)} copy(f32[2,3,192,512]{2,0,1,3:T(2,128)} %all-gather.2.cloned.1.call-done) | data formatting | bytes 4718592
  61.8 137.8 %while.19 = (s32[]{:T(128)}, f32[2,3,192,512]{3,2,1,0:T(8,128)S(1)}, f32[2,128,128]{2,1,0:T(8,128)S(1)}, s32[1,1,2]{2,1,0:T(1,128)S(1)}, s32[1,1,2]{2,1,0:T(1,12...) while((s32[]{:T(128)}, ...), condition=%wide.region_1.2_spmd.clone.clone.clone.clone, body=%wide.region_0.1_spmd.clone.clone.clone.clone.sunk | while | flops 2037301248 | bytes 20128300 | solution.py:133
  69.9 1.1 fusion.857
  75.0 0.8 fusion.868
  75.8 0.8 convolution_add_fusion.36
  77.1 0.8 fusion.866
  77.9 0.8 convolution_subtract_fusion.8
  79.6 1.5 multiply_add_fusion.7
  85.0 0.8 fusion.880
  85.9 1.3 convolution_add_fusion.37
  87.7 0.8 fusion.878
  88.5 0.8 convolution_subtract_fusion.10
  90.2 1.5 multiply_subtract_fusion.3
  99.3 1.5 add_bitcast_fusion.9
  105.1 0.8 fusion.902
  107.5 0.8 convolution_add_fusion.42
  109.8 1.5 add_bitcast_fusion.10
  115.5 0.8 fusion.913
  117.8 0.8 convolution_add_fusion.46
  120.4 1.5 add_bitcast_fusion.11
  122.1 2.3 dynamic_update_slice.36
  124.6 2.3 dynamic_update_slice.37
  127.0 2.3 dynamic_update_slice.38
  137.7 1.1 fusion.857
  142.7 0.8 fusion.868
  143.6 0.8 convolution_add_fusion.36
  144.8 0.8 fusion.866
  145.7 0.8 convolution_subtract_fusion.8
  147.4 1.5 multiply_add_fusion.7
  152.8 0.8 fusion.880
  153.6 1.0 convolution_add_fusion.37
  155.1 0.8 fusion.878
  155.9 0.8 convolution_subtract_fusion.10
  157.7 1.5 multiply_subtract_fusion.3
  166.7 1.5 add_bitcast_fusion.9
  172.6 0.8 fusion.902
  174.9 0.8 convolution_add_fusion.42
  177.3 1.5 add_bitcast_fusion.10
  183.0 0.8 fusion.913
  187.1 0.9 fusion.914
  188.1 1.5 add_bitcast_fusion.11
  189.8 2.3 dynamic_update_slice.36
  192.2 2.3 dynamic_update_slice.37
  194.6 2.3 dynamic_update_slice.38
  199.7 3.4 %copy.37 = f32[2,3,192,512]{2,1,0,3:T(4,128)} copy(f32[2,3,192,512]{3,2,1,0:T(8,128)S(1)} %get-tuple-element.508) | data formatting | bytes 4718592
  203.1 6.0 %reshape.42 = f32[512,1152]{1,0:T(8,128)} reshape(f32[512,2,3,192]{3,2,1,0:T(4,128)} %bitcast.367) | data formatting | bytes 4718592
  209.1 1.3 collective-permute-start.4
  210.5 4.1 %collective-permute-done.4 = f32[2,128,128]{2,1,0:T(8,128)S(1)} collective-permute-done((f32[2,128,128]{2,1,0:T(8,128)S(1)}, f32[2,128,128]{2,1,0:T(8,128)S(1)}, u32[]{:S(2)}, u32[]{:S(2)}) %collective-permute-start.4) | collective-permute-done | bytes 131104 | tf_op jit(solution)/shard_map/ppermute | solution.py:12
  214.5 2.3 collective-permute-start.5
  216.9 34.8 %reduce-scatter.4.cloned.1.call-done = f32[64,1152]{1,0:T(8,128)} async-done(((f32[512,1152]{1,0:T(8,128)}), f32[64,1152]{1,0:T(8,128)}) %reduce-scatter.4.cloned.1.call-update) | async-done | bytes 294928
  251.6 1.3 reshape.43
  253.5 1.3 collective-permute-start.3
  254.8 4.6 %collective-permute-start.2 = (f32[2,3,64,64]{3,2,1,0:T(8,128)S(1)}, f32[2,3,64,64]{3,2,1,0:T(8,128)S(1)}, u32[]{:S(2)}, u32[]{:S(2)}) collective-permute-start(f32[2,3,64,64]{3,2,1,0:T(8,128)S(1)} %copy.40), channel_id=1, source_target_pairs={{0,1},{1,2},{2,3},{4,5},{5,6},{6,7},{8,9},{9,10},{10,11},{12,13},{... | collective-permute-start | bytes 294920 | tf_op jit(solution)/shard_map/ppermute | solution.py:25
  260.2 1.7 collective-permute-done.3
  261.9 1.2 collective-permute-done.2
  263.7 49.0 %all-reduce.10.cloned.1.call-done = f32[2,128,128]{2,1,0:T(8,128)} async-done(((f32[2,128,128]{2,1,0:T(8,128)}), f32[2,128,128]{2,1,0:T(8,128)}) %all-reduce.10.cloned.1.call-update) | async-done | bytes 131088 | tf_op jit(solution)/shard_map/psum | solution.py:139
  312.7 1.6 copy.55
  (167 shorter events, 72.5 us)
Async XLA Ops:
  7.2 48.1 %all-gather.2.cloned.1.call-start = ((), (), s32[]{:S(2)}) async-start(), calls=%async_computation.1 | async-start | bytes 3538944 | tf_op jit(solution)/shard_map/all_gather | solution.py:88
  8.3 9.9 %collective-permute-start.1 = (f32[2,3,64,64]{2,0,1,3:T(2,128)S(1)}, f32[2,3,64,64]{2,0,1,3:T(2,128)S(1)}, u32[]{:S(2)}, u32[]{:S(2)}) collective-permute-start(f32[2,3,64,64]{2,0,1,3:T(2,128)S(1)} %copy.25), channel_id=1, source_target_pairs={{1,0},{2,1},{3,2},{5,4},{6,5},{7,6},{9,8},{10,9},{11,10},{13,12},{... | collective-permute-start | bytes 294920 | tf_op jit(solution)/shard_map/ppermute | solution.py:27
  9.6 9.7 %collective-permute-start = (f32[2,3,64,64]{2,0,1,3:T(2,128)S(1)}, f32[2,3,64,64]{2,0,1,3:T(2,128)S(1)}, u32[]{:S(2)}, u32[]{:S(2)}) collective-permute-start(f32[2,3,64,64]{2,0,1,3:T(2,128)S(1)} %copy.25), channel_id=1, source_target_pairs={{0,1},{1,2},{2,3},{4,5},{5,6},{6,7},{8,9},{9,10},{10,11},{12,13},{... | collective-permute-start | bytes 294920 | tf_op jit(solution)/shard_map/ppermute | solution.py:25
  20.6 231.1 %reduce-scatter.4.cloned.1.call-start = ((), (), s32[]{:S(2)}) async-start(), calls=%async_computation.3 | async-start | bytes 2654208
  60.8 0.9 copy-start
  60.8 0.9 copy-start.1
  60.8 0.9 copy-start.2
  60.8 0.9 copy-start.3
  60.8 1.0 copy-start.4
  209.1 103.6 %all-reduce.10.cloned.1.call-start = ((), (), s32[]{:S(2)}) async-start(), calls=%async_computation.2 | async-start | bytes 262144 | tf_op jit(solution)/shard_map/psum | solution.py:139
  209.1 5.4 %collective-permute-start.4 = (f32[2,128,128]{2,1,0:T(8,128)S(1)}, f32[2,128,128]{2,1,0:T(8,128)S(1)}, u32[]{:S(2)}, u32[]{:S(2)}) collective-permute-start(f32[2,128,128]{2,1,0:T(8,128)S(1)} %get-tuple-element.509), channel_id=1, source_target_pairs={{0,1},{1,0},{2,3},{3,2},{4,5},{5,4},{6,7},{7,6},{8,9},{9,8},{10,11... | collective-permute-start | bytes 393224 | tf_op jit(solution)/shard_map/ppermute | solution.py:12
  214.5 44.8 %collective-permute-start.5 = (f32[2,128,128]{2,1,0:T(8,128)S(1)}, f32[2,128,128]{2,1,0:T(8,128)S(1)}, u32[]{:S(2)}, u32[]{:S(2)}) collective-permute-start(f32[2,128,128]{2,1,0:T(8,128)S(1)} %add.635), channel_id=1, source_target_pairs={{0,2},{1,3},{2,0},{3,1},{4,6},{5,7},{6,4},{7,5},{8,10},{9,11},{10,... | collective-permute-start | bytes 393224 | tf_op jit(solution)/shard_map/ppermute | solution.py:12
  253.5 8.4 %collective-permute-start.3 = (f32[2,3,64,64]{3,2,1,0:T(8,128)S(1)}, f32[2,3,64,64]{3,2,1,0:T(8,128)S(1)}, u32[]{:S(2)}, u32[]{:S(2)}) collective-permute-start(f32[2,3,64,64]{3,2,1,0:T(8,128)S(1)} %copy.41), channel_id=1, source_target_pairs={{1,0},{2,1},{3,2},{5,4},{6,5},{7,6},{9,8},{10,9},{11,10},{13,12},{... | collective-permute-start | bytes 294920 | tf_op jit(solution)/shard_map/ppermute | solution.py:27
  254.8 8.3 %collective-permute-start.2 = (f32[2,3,64,64]{3,2,1,0:T(8,128)S(1)}, f32[2,3,64,64]{3,2,1,0:T(8,128)S(1)}, u32[]{:S(2)}, u32[]{:S(2)}) collective-permute-start(f32[2,3,64,64]{3,2,1,0:T(8,128)S(1)} %copy.40), channel_id=1, source_target_pairs={{0,1},{1,2},{2,3},{4,5},{5,6},{6,7},{8,9},{9,10},{10,11},{12,13},{... | collective-permute-start | bytes 294920 | tf_op jit(solution)/shard_map/ppermute | solution.py:25
Sparse Core Ops, SparseCore 0:
  20.7 34.4 all-gather.1
  209.2 42.3 reduce-scatter.3
  260.2 52.5 all-reduce.9
